TPU v7x, 64 devices: a 2x2x8 block of a 4x4x8 slice. The times are simulated.
64 devices in a mesh: rep: 8 (over x, y, core), dp: 8 (over z).
Axes of the slice: x: 2, y: 2, z: 8, core: 2. Of those that a mesh axis runs over, the one named last changes fastest.
The devices are a block of a 4x4x8 slice.
Arguments:
- a: bfloat16 [64, 4, 4096, 768], P(('rep', 'dp')), parts along dimension 0
- g: bfloat16 [64, 4, 4096, 3072], P(('rep', 'dp')), parts along dimension 0
Outputs:
- output: bfloat16 [32, 768, 3072], P('rep'), parts along dimension 0
There are 8 independent parts. A program takes and returns all parts, laid end to end along the dimension named above; each array names one.
All inputs are finite; a program needn't handle non-finite values.
Results may differ from a plain program's by a relative error of at most 0.012.
Values are sent between devices in bfloat16 or wider.
A program may use at most 768 MiB of HBM per device.

v0:
```python
import jax
import jax.numpy as jnp


def solution(mesh):
    groups = mesh.shape["rep"]

    def step(a, g):
        a, g = (t.reshape(groups, -1, *t.shape[1:]) for t in (a, g))
        sums = jnp.einsum("rsntd,rsntf->rndf", a, g, preferred_element_type=jnp.float32)
        return sums.astype(jnp.bfloat16).reshape(-1, *sums.shape[2:])

    return step
```

profile of v0, /device:TPU:21, one launch (start us, length us, event | category | flops | bytes accessed | tf_op | source)
XLA Modules:
  0.0 824.6 jit_solution(9256031216393629295)
XLA Ops:
  0.0 88.8 %fusion.3 = f32[1,4,768,3072]{3,2,1,0:T(8,128)} fusion(bf16[1,4,4096,3072]{3,2,1,0:T(8,128)(2,1)} %param.1, bf16[1,4,4096,768]{3,2,1,0:T(8,128)(2,1)} %param), kind=kOutput, calls=%fused_computation.4 | convolution fusion | flops 77309411328 | bytes 163577856 | tf_op jit(solution)/rsntd,rsntf->rndf/dot_general | solution.py:10
  88.8 735.8 %all-reduce.2 = bf16[1,4,768,3072]{3,2,1,0:T(8,128)(2,1)} all-reduce(f32[1,4,768,3072]{3,2,1,0:T(8,128)} %fusion.3), channel_id=1, replica_groups=[8,8]<=[64], use_global_device_ids=true, to_apply=%add.clone | all-reduce | flops 9437184 | bytes 56623104 | tf_op jit(solution)/rsntd,rsntf->rndf/dot_general | solution.py:10
where the time goes:
time: 825 us
  blocking collectives  736 us (89%)
  matrix products  88.8 us (11%)
    dot_general x1, blocking collectives, step(): jnp.einsum('rsntd,rsntf->rndf', a, g, preferred_element_type=jnp.float32)  736 us
    dot_general x1, matrix products, step(): jnp.einsum('rsntd,rsntf->rndf', a, g, preferred_element_type=jnp.float32)  88.8 us

commit v1 on v0

v1 whole, which is shorter than its diff:
```python
import functools

import jax
import jax.numpy as jnp
from jax import lax
from jax.experimental import pallas as pl
from jax.experimental.pallas import tpu as pltpu
from jax.sharding import PartitionSpec as P

MESH = pl.DeviceIdType.MESH
STREAMS = 2
PIECES = 4


def ring_kernel(
    size, a_hbm, g_hbm, sums, a_vmem, g_vmem, term, a_sem, g_sem, send_sem, recv_sem
):
    matrices, tokens, rows = a_hbm.shape
    columns = g_hbm.shape[2]
    half, width, piece = rows // 2, columns // size, tokens // PIECES
    rounds = matrices // STREAMS
    hops = 2 * (size - 1)
    per_round = hops * STREAMS
    halfsteps = rounds * per_round
    items = rounds * size * STREAMS

    me = lax.axis_index("dp")
    right, left = lax.rem(me + 1, size), lax.rem(me + size - 1, size)

    def place(h):
        r = lax.rem(h, per_round)
        x = lax.rem(r, STREAMS)
        return (h // per_round) * STREAMS + x, r // STREAMS, x

    def chunk(k, way):
        return lax.rem(me + 2 * size + (k if way else -k), size)

    def a_copy(n, x, j):
        part = pl.ds(pl.multiple_of(j * piece, piece), piece)
        return pltpu.make_async_copy(
            a_hbm.at[n, part, :], a_vmem.at[x, part, :], a_sem.at[x, j]
        )

    def g_copy(i, way, j):
        q, r = i // (size * STREAMS), lax.rem(i, size * STREAMS)
        n, k = q * STREAMS + lax.rem(r, STREAMS), r // STREAMS
        part = pl.ds(pl.multiple_of(j * piece, piece), piece)
        block = pl.ds(pl.multiple_of(chunk(k, way) * width, width), width)
        slot = lax.rem(i, 2)
        return pltpu.make_async_copy(
            g_hbm.at[n, part, block],
            g_vmem.at[slot, way, part, :],
            g_sem.at[slot, way, j],
        )

    def start_g(i):
        for j in range(PIECES):
            for way in range(2):
                g_copy(i, way, j).start()

    def view(n, k, way):
        block = pl.ds(pl.multiple_of(chunk(k, way) * width, width), width)
        return sums.at[n, pl.ds(way * half, half), block]

    def remote(h, way):
        n, k, _ = place(h)
        ref = view(n, k, way)
        return pltpu.make_async_remote_copy(
            src_ref=ref,
            dst_ref=ref,
            send_sem=send_sem.at[h, way],
            recv_sem=recv_sem.at[h, way],
            device_id={"dp": left if way else right},
            device_id_type=MESH,
        )

    for j in range(PIECES):
        a_copy(0, 0, j).start()
        for way in range(2):
            g_copy(0, way, j).start()

    barrier = pltpu.get_barrier_semaphore()
    for neighbour in (left, right):
        pl.semaphore_signal(
            barrier, inc=1, device_id={"dp": neighbour}, device_id_type=MESH
        )
    pl.semaphore_wait(barrier, 2)

    def communicate(h):
        n, k, _ = place(h)

        @pl.when(h >= STREAMS)
        def _():
            for way in range(2):
                remote(h - STREAMS, way).wait_recv()
            for way in range(2):
                remote(h - STREAMS, way).wait_send()

        @pl.when(k == 0)
        def _():
            for way in range(2):
                view(n, k, way)[...] = term[way].astype(sums.dtype)

        @pl.when((k > 0) & (k < size))
        def _():
            for way in range(2):
                ref = view(n, k, way)
                ref[...] = (ref[...].astype(jnp.float32) + term[way]).astype(sums.dtype)

        for way in range(2):
            remote(h, way).start()

    def compute(h):
        n, k, x = place(h)
        q = n // STREAMS
        i = q * size * STREAMS + k * STREAMS + x
        slot = lax.rem(i, 2)
        term[...] = jnp.zeros_like(term)

        @pl.loop(0, PIECES)
        def _(j):
            @pl.when(k == 0)
            def _():
                a_copy(n, x, j).wait()

            for way in range(2):
                g_copy(i, way, j).wait()

            @pl.when((j == 2) & (i + 1 < items))
            def _():
                start_g(i + 1)

            @pl.when((j == 2) & (i == 0))
            def _():
                for x1 in range(1, STREAMS):
                    for j1 in range(PIECES):
                        a_copy(x1, x1, j1).start()

            part = pl.ds(pl.multiple_of(j * piece, piece), piece)
            for way in range(2):
                term[way] += lax.dot_general(
                    a_vmem[x, part, way * half : (way + 1) * half],
                    g_vmem[slot, way, part, :],
                    (((0,), (0,)), ((), ())),
                    preferred_element_type=jnp.float32,
                )

        @pl.when((k == size - 1) & (q < rounds - 1))
        def _():
            for j in range(PIECES):
                a_copy(n + STREAMS, x, j).start()

    @pl.loop(0, halfsteps + 1)
    def _(t):
        @pl.when(t > 0)
        def _():
            communicate(t - 1)

        @pl.when((t < halfsteps) & (lax.rem(t, per_round) // STREAMS < size))
        def _():
            compute(t)

    for h in range(halfsteps - STREAMS, halfsteps):
        for way in range(2):
            remote(h, way).wait_recv()
        for way in range(2):
            remote(h, way).wait_send()


def solution(mesh):
    size = mesh.shape["dp"]

    def step(a, g):
        a, g = a[0], g[0]
        matrices, tokens, rows = a.shape
        columns = g.shape[2]
        half, width = rows // 2, columns // size
        halfsteps = matrices * 2 * (size - 1)
        shape = (matrices, rows, columns)
        return pl.pallas_call(
            functools.partial(ring_kernel, size),
            out_shape=pltpu.VMEM(shape, jnp.bfloat16),
            in_specs=[pl.BlockSpec(memory_space=pltpu.HBM)] * 2,
            out_specs=pl.BlockSpec(memory_space=pltpu.VMEM),
            scratch_shapes=[
                pltpu.VMEM((STREAMS, tokens, rows), jnp.bfloat16),
                pltpu.VMEM((2, 2, tokens, width), jnp.bfloat16),
                pltpu.VMEM((2, half, width), jnp.float32),
                pltpu.SemaphoreType.DMA((STREAMS, PIECES)),
                pltpu.SemaphoreType.DMA((2, 2, PIECES)),
                pltpu.SemaphoreType.DMA((halfsteps, 2)),
                pltpu.SemaphoreType.DMA((halfsteps, 2)),
            ],
            compiler_params=pltpu.CompilerParams(
                collective_id=0,
                has_side_effects=True,
                vmem_limit_bytes=36 * 1024 * 1024,
            ),
            cost_estimate=pl.CostEstimate(
                flops=2 * matrices * tokens * rows * columns,
                bytes_accessed=2 * matrices * tokens * (rows + 2 * columns),
                transcendentals=0,
            ),
        )(a, g)

    return jax.shard_map(
        step,
        mesh=mesh,
        in_specs=(P(("rep", "dp")), P(("rep", "dp"))),
        out_specs=P("rep"),
        check_vma=False,
    )
```

time: 825 us -> 378 us (0.46)
  blocking collectives: 736 us -> 0 us
  Pallas kernels: 0 us -> 371 us
  matrix products: 88.8 us -> 0 us
    dot_general x1 -> x0, blocking collectives: 736 us -> none  [step(): jnp.einsum('rsntd,rsntf->rndf', a, g, preferred_element_type=jnp.float32)]
    pallas_call x0 -> x1, Pallas kernels: none -> 371 us  [step(): pl.pallas_call(functools.partial(ring_kernel, size), out_shape=pltpu.VMEM...]
    dot_general x1 -> x0, matrix products: 88.8 us -> none  [step(): jnp.einsum('rsntd,rsntf->rndf', a, g, preferred_element_type=jnp.float32)]
where the time goes in v1:
time: 378 us
  Pallas kernels  371 us (98%)
  local copies, waits for them, and re-layouts  6.85 us (2%)
    pallas_call x1, Pallas kernels, step(): pl.pallas_call(functools.partial(ring_kernel, size), out_shape=pltpu.VMEM...  371 us

profile of v1, /device:TPU:21, one launch (start us, length us, event | category | flops | bytes accessed | tf_op | source)
XLA Modules:
  0.0 378.1 jit_solution(421152054458820293)
XLA Ops:
  0.0 371.3 %shard_map.28 = bf16[4,768,3072]{2,1,0:T(8,128)(2,1)S(1)} custom-call(bf16[4,4096,768]{2,1,0:T(8,128)(2,1)} %bitcast.2, bf16[4,4096,3072]{2,1,0:T(8,128)(2,1)} %bitcast.1.g_hbm), custom_call_target="tpu_custom_call" | custom-call | flops 77309411328 | bytes 226492416 | tf_op jit(solution)/shard_map/pallas_call | solution.py:180
  371.3 6.9 %copy.4 = bf16[4,768,3072]{2,1,0:T(8,128)(2,1)} copy(bf16[4,768,3072]{2,1,0:T(8,128)(2,1)S(1)} %shard_map.28) | data formatting | bytes 37748736

commit v2 on v1

v2 whole, which is shorter than its diff:
```python
import functools

import jax
import jax.numpy as jnp
from jax import lax
from jax.experimental import pallas as pl
from jax.experimental.pallas import tpu as pltpu
from jax.sharding import PartitionSpec as P

MESH = pl.DeviceIdType.MESH
STREAMS = 2
JOINED = 2
PIECES = 4
STRIP = 128


def ring_kernel(
    size, a_hbm, g_hbm, sums, a_vmem, g_vmem, term, a_sem, g_sem, send_sem, recv_sem
):
    matrices, tokens, rows = a_hbm.shape
    columns = g_hbm.shape[2]
    strips, width, piece = rows // (2 * STRIP), columns // size, tokens // PIECES
    rounds = matrices // STREAMS
    per_round = 2 * (size - 1) * STREAMS
    halfsteps = rounds * per_round
    items = rounds * size * STREAMS
    parts = [(s, 0, width) for s in range(strips)]

    me = lax.axis_index("dp")
    right, left = lax.rem(me + 1, size), lax.rem(me + size - 1, size)

    def place(h):
        r = lax.rem(h, per_round)
        x = lax.rem(r, STREAMS)
        return (h // per_round) * STREAMS + x, r // STREAMS, x

    def block(k, way, first=0, last=width):
        c = lax.rem(me + 2 * size + (k if way else -k), size)
        return pl.ds(pl.multiple_of(c * width + first, STRIP), last - first)

    def tokens_of(j):
        return pl.ds(pl.multiple_of(j * piece, piece), piece)

    def a_copy(n, x, j):
        return pltpu.make_async_copy(
            a_hbm.at[n, tokens_of(j), :], a_vmem.at[x, tokens_of(j), :], a_sem.at[x, j]
        )

    def first_a_copy(s, j):
        strip = pl.ds(2 * STRIP * s, 2 * STRIP)
        return pltpu.make_async_copy(
            a_hbm.at[0, tokens_of(j), strip],
            a_vmem.at[0, tokens_of(j), strip],
            a_sem.at[s + STREAMS - 1 if s else 0, j],
        )

    def first_g_copy(p, j):
        _, first, last = parts[p]
        return pltpu.make_async_copy(
            g_hbm.at[0, tokens_of(j), block(0, 0, first, last)],
            g_vmem.at[0, 0, tokens_of(j), pl.ds(first, last - first)],
            g_sem.at[0, 0, j],
        )

    def item_place(i):
        q, r = i // (size * STREAMS), lax.rem(i, size * STREAMS)
        return q * STREAMS + lax.rem(r, STREAMS), r // STREAMS

    def g_copy(i, way, j):
        n, k = item_place(i)
        slot = lax.rem(i, 2)
        return pltpu.make_async_copy(
            g_hbm.at[n, tokens_of(j), block(k, way)],
            g_vmem.at[slot, way, tokens_of(j), :],
            g_sem.at[slot, way, j],
        )

    def apart(k):
        return (lax.rem(k, size // 2) + size // 2 - 1) // (size // 2)

    def start_g(i):
        _, k = item_place(i)
        for j in range(PIECES):
            g_copy(i, 0, j).start()

            @pl.when(apart(k) == 1)
            def _():
                g_copy(i, 1, j).start()

    def remote(h, way):
        n, k, _ = place(h)
        ref = sums.at[n, :, way, :, block(k, way)]
        sem = lax.rem(h, 2 * STREAMS)
        return pltpu.make_async_remote_copy(
            src_ref=ref,
            dst_ref=ref,
            send_sem=send_sem.at[sem, way],
            recv_sem=recv_sem.at[sem, way],
            device_id={"dp": left if way else right},
            device_id_type=MESH,
        )

    def remote_part(p, way):
        s, first, last = parts[p]
        ref = sums.at[0, s, way, :, block(0, way, first, last)]
        sem = 2 * STREAMS + p
        return pltpu.make_async_remote_copy(
            src_ref=ref,
            dst_ref=ref,
            send_sem=send_sem.at[sem, way],
            recv_sem=recv_sem.at[sem, way],
            device_id={"dp": left if way else right},
            device_id_type=MESH,
        )

    def matmul(lhs, rhs):
        return lax.dot_general(
            lhs, rhs, (((0,), (0,)), ((), ())), preferred_element_type=jnp.float32
        )

    def compute_part(s):
        strip = slice(2 * STRIP * s, 2 * STRIP * (s + 1))
        if s == 0:
            term[:, 0] = jnp.zeros((2, STRIP, width), jnp.float32)

            @pl.loop(0, PIECES)
            def _(j):
                first_a_copy(0, j).wait()
                first_g_copy(0, j).wait()

                @pl.when(j == 1)
                def _():
                    for s1 in range(1, strips):
                        for j1 in range(PIECES):
                            first_a_copy(s1, j1).start()

                @pl.when(j == PIECES - 1)
                def _():
                    for j1 in range(PIECES):
                        for x in range(1, STREAMS):
                            a_copy(x, x, j1).start()
                        g_copy(1, 0, j1).start()

                product = matmul(
                    a_vmem[0, tokens_of(j), strip], g_vmem[0, 0, tokens_of(j), :]
                )
                term[:, 0] += product.reshape(2, STRIP, width)

        else:
            for j in range(PIECES):
                first_a_copy(s, j).wait()
            product = matmul(a_vmem[0, :, strip], g_vmem[0, 0])
            term[:, s] = product.reshape(2, STRIP, width)
        for way in range(2):
            sums[0, s, way, :, block(0, way)] = term[way, s].astype(sums.dtype)

    def communicate(h):
        n, k, _ = place(h)

        @pl.when(h == STREAMS)
        def _():
            for p in range(len(parts)):
                for way in range(2):
                    remote_part(p, way).wait()

        @pl.when(h > STREAMS)
        def _():
            for way in range(2):
                remote(h - STREAMS, way).wait()

        @pl.when(k == 0)
        def _():
            for way in range(2):
                sums[n, :, way, :, block(k, way)] = term[way].astype(sums.dtype)

        @pl.when((k > 0) & (k < size))
        def _():
            for way in range(2):
                cols = block(k, way)
                came = sums[n, :, way, :, cols].astype(jnp.float32)
                sums[n, :, way, :, cols] = (came + term[way]).astype(sums.dtype)

        for way in range(2):
            remote(h, way).start()

    def compute(h):
        n, k, x = place(h)
        q = n // STREAMS
        i = q * size * STREAMS + k * STREAMS + x
        slot = lax.rem(i, 2)
        term[...] = jnp.zeros_like(term)

        @pl.loop(0, PIECES // JOINED)
        def _(jj):
            for j in range(JOINED):
                load = jj * JOINED + j

                @pl.when(k == 0)
                def _():
                    a_copy(n, x, load).wait()

                g_copy(i, 0, load).wait()

                @pl.when(apart(k) == 1)
                def _():
                    g_copy(i, 1, load).wait()

            @pl.when((jj == 0) & (i + 1 < items))
            def _():
                start_g(i + 1)

            part = pl.ds(pl.multiple_of(jj * JOINED * piece, piece), JOINED * piece)
            lhs = a_vmem[x, part, :]
            for way in range(2):
                strip = [
                    lhs[:, (2 * s + way) * STRIP : (2 * s + way + 1) * STRIP]
                    for s in range(strips)
                ]
                product = matmul(
                    jnp.concatenate(strip, axis=1),
                    g_vmem[slot, way * apart(k), part, :],
                )
                term[way] += product.reshape(strips, STRIP, width)

        @pl.when((k == size - 1) & (q < rounds - 1))
        def _():
            for j in range(PIECES):
                a_copy(n + STREAMS, x, j).start()

    barrier = pltpu.get_barrier_semaphore()
    for neighbour in (left, right):
        pl.semaphore_signal(
            barrier, inc=1, device_id={"dp": neighbour}, device_id_type=MESH
        )
    for j in range(PIECES):
        first_a_copy(0, j).start()
        first_g_copy(0, j).start()
    for p in range(len(parts)):
        compute_part(p)
        if p == 0:
            pl.semaphore_wait(barrier, 2)
        for way in range(2):
            remote_part(p, way).start()

    @pl.loop(1, halfsteps + 1)
    def _(t):
        @pl.when(t > 1)
        def _():
            communicate(t - 1)

        @pl.when((t < halfsteps) & (lax.rem(t, per_round) // STREAMS < size))
        def _():
            compute(t)

    for h in range(halfsteps - STREAMS, halfsteps):
        for way in range(2):
            remote(h, way).wait()


def store_kernel(sums, out, sem):
    copies = [
        pltpu.make_async_copy(sums.at[n], out.at[n], sem.at[n])
        for n in range(sums.shape[0])
    ]
    for copy in copies:
        copy.start()
    for copy in copies:
        copy.wait()


def solution(mesh):
    size = mesh.shape["dp"]

    def step(a, g):
        a, g = a[0], g[0]
        matrices, tokens, rows = a.shape
        columns = g.shape[2]
        strips, width = rows // (2 * STRIP), columns // size
        parts = strips
        shape = (matrices, strips, 2, STRIP, columns)
        sums = pl.pallas_call(
            functools.partial(ring_kernel, size),
            out_shape=pltpu.VMEM(shape, jnp.bfloat16),
            in_specs=[pl.BlockSpec(memory_space=pltpu.HBM)] * 2,
            out_specs=pl.BlockSpec(memory_space=pltpu.VMEM),
            scratch_shapes=[
                pltpu.VMEM((STREAMS, tokens, rows), jnp.bfloat16),
                pltpu.VMEM((2, 2, tokens, width), jnp.bfloat16),
                pltpu.VMEM((2, strips, STRIP, width), jnp.float32),
                pltpu.SemaphoreType.DMA((STREAMS + strips - 1, PIECES)),
                pltpu.SemaphoreType.DMA((2, 2, PIECES)),
                pltpu.SemaphoreType.DMA((2 * STREAMS + parts, 2)),
                pltpu.SemaphoreType.DMA((2 * STREAMS + parts, 2)),
            ],
            compiler_params=pltpu.CompilerParams(
                collective_id=0,
                has_side_effects=True,
                vmem_limit_bytes=36 * 1024 * 1024,
            ),
            cost_estimate=pl.CostEstimate(
                flops=2 * matrices * tokens * rows * columns,
                bytes_accessed=2 * matrices * tokens * (rows + 2 * columns),
                transcendentals=0,
            ),
        )(a, g)
        out = pl.pallas_call(
            store_kernel,
            out_shape=jax.ShapeDtypeStruct(shape, jnp.bfloat16),
            in_specs=[pl.BlockSpec(memory_space=pltpu.VMEM)],
            out_specs=pl.BlockSpec(memory_space=pltpu.HBM),
            scratch_shapes=[pltpu.SemaphoreType.DMA((matrices,))],
            compiler_params=pltpu.CompilerParams(vmem_limit_bytes=20 * 1024 * 1024),
        )(sums)
        return out.reshape(matrices, rows, columns)

    return jax.shard_map(
        step,
        mesh=mesh,
        in_specs=(P(("rep", "dp")), P(("rep", "dp"))),
        out_specs=P("rep"),
        check_vma=False,
    )
```

time: 378 us -> 373 us (0.987)
  local copies, waits for them, and re-layouts: 6.85 us -> 0 us
    unnamed x1 -> x0, local copies, waits for them, and re-layouts: 6.85 us -> none
    pallas_call x0 -> x1, Pallas kernels: none -> 6.61 us  [step(): pl.pallas_call(store_kernel, out_shape=jax.ShapeDtypeStruct(shape, jnp.bf...]
    pallas_call x1, Pallas kernels: 371 us -> 367 us  [step(): pl.pallas_call(functools.partial(ring_kernel, size), out_shape=pltpu.VMEM...]
where the time goes in v2:
time: 373 us
  Pallas kernels  373 us (100%)
    pallas_call x1, Pallas kernels, step(): pl.pallas_call(functools.partial(ring_kernel, size), out_shape=pltpu.VMEM...  367 us

profile of v2, /device:TPU:21, one launch (start us, length us, event | category | flops | bytes accessed | tf_op | source)
XLA Modules:
  0.0 373.3 jit_solution(13849069351704844307)
XLA Ops:
  0.0 366.7 %shard_map.28.sums = bf16[4,3,2,128,3072]{4,3,2,1,0:T(8,128)(2,1)S(1)} custom-call(bf16[4,4096,768]{2,1,0:T(8,128)(2,1)} %bitcast.3, bf16[4,4096,3072]{2,1,0:T(8,128)(2,1)} %bitcast.1.g_hbm), custom_call_target="tpu_custom_call" | custom-call | flops 77309411328 | bytes 226492416 | tf_op jit(solution)/shard_map/pallas_call | solution.py:281
  366.7 6.6 %shard_map.29 = bf16[4,3,2,128,3072]{4,3,2,1,0:T(8,128)(2,1)} custom-call(bf16[4,3,2,128,3072]{4,3,2,1,0:T(8,128)(2,1)S(1)} %shard_map.28.sums), custom_call_target="tpu_custom_call" | custom-call | tf_op jit(solution)/shard_map/pallas_call | solution.py:306

commit v3 on v2

v3 whole, which is shorter than its diff:
```python
import functools

import jax
import jax.numpy as jnp
from jax import lax
from jax.experimental import pallas as pl
from jax.experimental.pallas import tpu as pltpu
from jax.sharding import PartitionSpec as P

MESH = pl.DeviceIdType.MESH
STREAMS = 2
HALVES = 2
PIECES = 4
STRIP = 128


def ring_kernel(
    size,
    a_hbm,
    g_hbm,
    sums,
    a_vmem,
    g_vmem,
    term,
    first_sem,
    strip_sem,
    a_sem,
    g_sem,
    send_sem,
    recv_sem,
):
    matrices, tokens, rows = a_hbm.shape
    columns = g_hbm.shape[2]
    strips, width = rows // (2 * STRIP), columns // size
    rounds = matrices // STREAMS
    per_round = 2 * (size - 1) * STREAMS
    halfsteps = rounds * per_round
    items = rounds * size * STREAMS
    me = lax.axis_index("dp")
    right, left = lax.rem(me + 1, size), lax.rem(me + size - 1, size)

    def place(h):
        r = lax.rem(h, per_round)
        x = lax.rem(r, STREAMS)
        return (h // per_round) * STREAMS + x, r // STREAMS, x

    def block(k, way, first=0, last=width):
        c = lax.rem(me + 2 * size + (k if way else -k), size)
        return pl.ds(pl.multiple_of(c * width + first, STRIP), last - first)

    def tokens_of(j, count):
        part = tokens // count
        return pl.ds(pl.multiple_of(j * part, part), part)

    def a_copy(n, x, j):
        part = tokens_of(j, HALVES)
        return pltpu.make_async_copy(
            a_hbm.at[n, part, :], a_vmem.at[x, part, :], a_sem.at[x, j]
        )

    def strip_of(s):
        return pl.ds(pl.multiple_of(2 * STRIP * s, 2 * STRIP), 2 * STRIP)

    def first_copies(j):
        part = tokens_of(j, PIECES)
        return (
            pltpu.make_async_copy(
                a_hbm.at[0, part, strip_of(0)],
                a_vmem.at[0, part, strip_of(0)],
                first_sem.at[0, j],
            ),
            pltpu.make_async_copy(
                g_hbm.at[0, part, block(0, 0, 0, STRIP)],
                g_vmem.at[0, 0, part, pl.ds(0, STRIP)],
                first_sem.at[1, j],
            ),
        )

    def first_g_copy():
        return pltpu.make_async_copy(
            g_hbm.at[0, :, block(0, 0, STRIP, width)],
            g_vmem.at[0, 0, :, pl.ds(STRIP, width - STRIP)],
            g_sem.at[0, 0, 0],
        )

    def first_a_copy(s):
        return pltpu.make_async_copy(
            a_hbm.at[0, :, strip_of(s)], a_vmem.at[0, :, strip_of(s)], strip_sem.at[s]
        )

    def item_place(i):
        q, r = i // (size * STREAMS), lax.rem(i, size * STREAMS)
        return q * STREAMS + lax.rem(r, STREAMS), r // STREAMS

    def g_copy(i, way, j):
        n, k = item_place(i)
        slot = lax.rem(i, 2)
        return pltpu.make_async_copy(
            g_hbm.at[n, tokens_of(j, HALVES), block(k, way)],
            g_vmem.at[slot, way, tokens_of(j, HALVES), :],
            g_sem.at[slot, way, j],
        )

    def apart(k):
        return (lax.rem(k, size // 2) + size // 2 - 1) // (size // 2)

    def start_g(i):
        _, k = item_place(i)
        for j in range(HALVES):
            g_copy(i, 0, j).start()

            @pl.when(apart(k) == 1)
            def _():
                g_copy(i, 1, j).start()

    def remote(h, way):
        n, k, _ = place(h)
        ref = sums.at[n, :, way, :, block(k, way)]
        sem = lax.rem(h, 2 * STREAMS)
        return pltpu.make_async_remote_copy(
            src_ref=ref,
            dst_ref=ref,
            send_sem=send_sem.at[sem, way],
            recv_sem=recv_sem.at[sem, way],
            device_id={"dp": left if way else right},
            device_id_type=MESH,
        )

    def remote_part(r, way, first=0, last=width):
        x, s = r // strips, lax.rem(r, strips)
        ref = sums.at[x, s, way, :, block(0, way, first, last)]
        return pltpu.make_async_remote_copy(
            src_ref=ref,
            dst_ref=ref,
            send_sem=send_sem.at[x, way],
            recv_sem=recv_sem.at[x, way],
            device_id={"dp": left if way else right},
            device_id_type=MESH,
        )

    def matmul(lhs, rhs):
        return lax.dot_general(
            lhs, rhs, (((0,), (0,)), ((), ())), preferred_element_type=jnp.float32
        )

    def send_part(r, first=0, last=width):
        x, s = r // strips, lax.rem(r, strips)
        for way in range(2):
            sums[x, s, way, :, block(0, way, first, last)] = term[
                way, s, :, first:last
            ].astype(sums.dtype)
        for way in range(2):
            remote_part(r, way, first, last).start()

    def first_strip():
        shape = (2, STRIP, STRIP)
        term[:, 0, :, :STRIP] = jnp.zeros(shape, jnp.float32)

        @pl.loop(0, PIECES)
        def _(j):
            for copy in first_copies(j):
                copy.wait()

            @pl.when(j == 0)
            def _():
                first_g_copy().start()

            @pl.when(j == 2)
            def _():
                for s in range(1, strips):
                    first_a_copy(s).start()

            part = tokens_of(j, PIECES)
            product = matmul(
                a_vmem[0, part, : 2 * STRIP], g_vmem[0, 0, part, :STRIP]
            )
            term[:, 0, :, :STRIP] += product.reshape(shape)

        pl.semaphore_wait(barrier, 2)
        send_part(0, 0, STRIP)

        for x in range(1, STREAMS):
            for j in range(HALVES):
                a_copy(x, x, j).start()
                g_copy(x, 0, j).start()

        first_g_copy().wait()
        product = matmul(a_vmem[0, :, : 2 * STRIP], g_vmem[0, 0, :, STRIP:])
        term[:, 0, :, STRIP:] = product.reshape(2, STRIP, width - STRIP)
        send_part(0, STRIP, width)

    def next_strip(r):
        x, s = r // strips, lax.rem(r, strips)

        @pl.when(x == 0)
        def _():
            first_a_copy(s).wait()

        @pl.when((x > 0) & (s == 0))
        def _():
            for j in range(HALVES):
                a_copy(x, x, j).wait()
                g_copy(x, 0, j).wait()

        strip = strip_of(s)
        product = matmul(a_vmem[x, :, strip], g_vmem[lax.rem(x, 2), 0])
        term[:, s] = product.reshape(2, STRIP, width)
        send_part(r)

        @pl.when(r == strips - 1)
        def _():
            start_g(2)

    def communicate(h):
        n, k, _ = place(h)

        for way in range(2):
            remote(h - STREAMS, way).wait()

        @pl.when(k == 0)
        def _():
            for way in range(2):
                sums[n, :, way, :, block(k, way)] = term[way].astype(sums.dtype)

        @pl.when((k > 0) & (k < size))
        def _():
            for way in range(2):
                cols = block(k, way)
                came = sums[n, :, way, :, cols].astype(jnp.float32)
                sums[n, :, way, :, cols] = (came + term[way]).astype(sums.dtype)

        for way in range(2):
            remote(h, way).start()

    def compute(h):
        n, k, x = place(h)
        q = n // STREAMS
        i = q * size * STREAMS + k * STREAMS + x
        slot = lax.rem(i, 2)
        term[...] = jnp.zeros_like(term)

        @pl.loop(0, HALVES)
        def _(j):
            @pl.when(k == 0)
            def _():
                a_copy(n, x, j).wait()

            g_copy(i, 0, j).wait()

            @pl.when(apart(k) == 1)
            def _():
                g_copy(i, 1, j).wait()

            @pl.when((j == 0) & (i + 1 < items))
            def _():
                start_g(i + 1)

            part = tokens_of(j, HALVES)
            lhs = a_vmem[x, part, :]
            for way in range(2):
                strip = [
                    lhs[:, (2 * s + way) * STRIP : (2 * s + way + 1) * STRIP]
                    for s in range(strips)
                ]
                product = matmul(
                    jnp.concatenate(strip, axis=1),
                    g_vmem[slot, way * apart(k), part, :],
                )
                term[way] += product.reshape(strips, STRIP, width)

        @pl.when((k == size - 1) & (q < rounds - 1))
        def _():
            for j in range(HALVES):
                a_copy(n + STREAMS, x, j).start()

    barrier = pltpu.get_barrier_semaphore()
    for neighbour in (left, right):
        pl.semaphore_signal(
            barrier, inc=1, device_id={"dp": neighbour}, device_id_type=MESH
        )
    for j in range(PIECES):
        for copy in first_copies(j):
            copy.start()
    first_strip()
    pl.loop(1, STREAMS * strips)(next_strip)

    @pl.loop(STREAMS, halfsteps + 1)
    def _(t):
        @pl.when(t > STREAMS)
        def _():
            communicate(t - 1)

        @pl.when((t < halfsteps) & (lax.rem(t, per_round) // STREAMS < size))
        def _():
            compute(t)

    for h in range(halfsteps - STREAMS, halfsteps):
        for way in range(2):
            remote(h, way).wait()


def store_kernel(sums, out, sem):
    copies = [
        pltpu.make_async_copy(sums.at[n, s], out.at[n, s], sem.at[n, s])
        for n in range(sums.shape[0])
        for s in range(sums.shape[1])
    ]
    for copy in copies:
        copy.start()
    for copy in copies:
        copy.wait()


def solution(mesh):
    size = mesh.shape["dp"]

    def step(a, g):
        a, g = a[0], g[0]
        matrices, tokens, rows = a.shape
        columns = g.shape[2]
        strips, width = rows // (2 * STRIP), columns // size
        shape = (matrices, strips, 2, STRIP, columns)
        sums = pl.pallas_call(
            functools.partial(ring_kernel, size),
            out_shape=pltpu.VMEM(shape, jnp.bfloat16),
            in_specs=[pl.BlockSpec(memory_space=pltpu.HBM)] * 2,
            out_specs=pl.BlockSpec(memory_space=pltpu.VMEM),
            scratch_shapes=[
                pltpu.VMEM((STREAMS, tokens, rows), jnp.bfloat16),
                pltpu.VMEM((2, 2, tokens, width), jnp.bfloat16),
                pltpu.VMEM((2, strips, STRIP, width), jnp.float32),
                pltpu.SemaphoreType.DMA((2, PIECES)),
                pltpu.SemaphoreType.DMA((strips,)),
                pltpu.SemaphoreType.DMA((STREAMS, HALVES)),
                pltpu.SemaphoreType.DMA((2, 2, HALVES)),
                pltpu.SemaphoreType.DMA((2 * STREAMS, 2)),
                pltpu.SemaphoreType.DMA((2 * STREAMS, 2)),
            ],
            compiler_params=pltpu.CompilerParams(
                collective_id=0,
                has_side_effects=True,
                vmem_limit_bytes=36 * 1024 * 1024,
            ),
            cost_estimate=pl.CostEstimate(
                flops=2 * matrices * tokens * rows * columns,
                bytes_accessed=2 * matrices * tokens * (rows + 2 * columns),
                transcendentals=0,
            ),
        )(a, g)
        out = pl.pallas_call(
            store_kernel,
            out_shape=jax.ShapeDtypeStruct(shape, jnp.bfloat16),
            in_specs=[pl.BlockSpec(memory_space=pltpu.VMEM)],
            out_specs=pl.BlockSpec(memory_space=pltpu.HBM),
            scratch_shapes=[pltpu.SemaphoreType.DMA((matrices, strips))],
            compiler_params=pltpu.CompilerParams(vmem_limit_bytes=20 * 1024 * 1024),
        )(sums)
        return out.reshape(matrices, rows, columns)

    return jax.shard_map(
        step,
        mesh=mesh,
        in_specs=(P(("rep", "dp")), P(("rep", "dp"))),
        out_specs=P("rep"),
        check_vma=False,
    )
```

time: 373 us -> 372 us (level)
  no operation moved by 1% of the time
where the time goes in v3:
time: 372 us
  Pallas kernels  372 us (100%)
    pallas_call x1, Pallas kernels, step(): pl.pallas_call(functools.partial(ring_kernel, size), out_shape=pltpu.VMEM...  366 us

profile of v3, /device:TPU:21, one launch (start us, length us, event | category | flops | bytes accessed | tf_op | source)
XLA Modules:
  0.0 372.4 jit_solution(3744067517042561960)
XLA Ops:
  0.0 365.8 %shard_map.28.sums = bf16[4,3,2,128,3072]{4,3,2,1,0:T(8,128)(2,1)S(1)} custom-call(bf16[4,4096,768]{2,1,0:T(8,128)(2,1)} %bitcast.3, bf16[4,4096,3072]{2,1,0:T(8,128)(2,1)} %bitcast.1.g_hbm), custom_call_target="tpu_custom_call" | custom-call | flops 77309411328 | bytes 226492416 | tf_op jit(solution)/shard_map/pallas_call | solution.py:323
  365.8 6.6 %shard_map.29 = bf16[4,3,2,128,3072]{4,3,2,1,0:T(8,128)(2,1)} custom-call(bf16[4,3,2,128,3072]{4,3,2,1,0:T(8,128)(2,1)S(1)} %shard_map.28.sums), custom_call_target="tpu_custom_call" | custom-call | tf_op jit(solution)/shard_map/pallas_call | solution.py:350

commit v4 on v3

--- a/solution.py
+++ b/solution.py
@@ -273,14 +273,14 @@
             for j in range(HALVES):
                 a_copy(n + STREAMS, x, j).start()
 
+    for j in range(PIECES):
+        for copy in first_copies(j):
+            copy.start()
     barrier = pltpu.get_barrier_semaphore()
     for neighbour in (left, right):
         pl.semaphore_signal(
             barrier, inc=1, device_id={"dp": neighbour}, device_id_type=MESH
         )
-    for j in range(PIECES):
-        for copy in first_copies(j):
-            copy.start()
     first_strip()
     pl.loop(1, STREAMS * strips)(next_strip)
 

time: 372 us -> 372 us (level)
  no operation moved by 1% of the time
where the time goes in v4:
time: 372 us
  Pallas kernels  372 us (100%)
    pallas_call x1, Pallas kernels, step(): pl.pallas_call(functools.partial(ring_kernel, size), out_shape=pltpu.VMEM...  366 us

profile of v4, /device:TPU:21, one launch (start us, length us, event | category | flops | bytes accessed | tf_op | source)
XLA Modules:
  0.0 372.4 jit_solution(4912105620391203996)
XLA Ops:
  0.0 365.8 %shard_map.28.sums = bf16[4,3,2,128,3072]{4,3,2,1,0:T(8,128)(2,1)S(1)} custom-call(bf16[4,4096,768]{2,1,0:T(8,128)(2,1)} %bitcast.3, bf16[4,4096,3072]{2,1,0:T(8,128)(2,1)} %bitcast.1.g_hbm), custom_call_target="tpu_custom_call" | custom-call | flops 77309411328 | bytes 226492416 | tf_op jit(solution)/shard_map/pallas_call | solution.py:323
  365.8 6.6 %shard_map.29 = bf16[4,3,2,128,3072]{4,3,2,1,0:T(8,128)(2,1)} custom-call(bf16[4,3,2,128,3072]{4,3,2,1,0:T(8,128)(2,1)S(1)} %shard_map.28.sums), custom_call_target="tpu_custom_call" | custom-call | tf_op jit(solution)/shard_map/pallas_call | solution.py:350
